TPU v7x, 32 devices: a whole 2x2x4 slice. The times are simulated.
32 devices in a mesh: dp: 4 (over x, core), pp: 8 (over z, y).
Axes of the slice: x: 2, y: 2, z: 4, core: 2. Of those that a mesh axis runs over, the one named last changes fastest.
Arguments:
- hidden: bfloat16 [512, 4096], P(('dp', 'pp')), may hold values from -400 to 400
- norm_gain: float32 [4096], replicated, may hold values from 0.1 to 1.9
- head: bfloat16 [32768, 4096], P(('dp', 'pp')), may hold values from -32 to 32
- targets: int32 [512], P(('dp', 'pp')), may hold values from 0 to 32767
- route: int32 [32], replicated, may hold values from 0 to 3
Outputs:
- token_loss: float32 [512], P(('dp', 'pp'))
- pipe_loss: float32 [4], replicated
All inputs are finite; a program needn't handle non-finite values.
Results may differ from a plain program's by a relative error of at most 0.00053.
Values may be sent and summed in bfloat16 or wider, within the bound.
A program may use at most 64 MiB of HBM per device.

v0:
```python
import math
import jax
import jax.numpy as jnp
from jax import lax
from jax.sharding import PartitionSpec as P


def rms_normal(rows, gain):
    wide = rows.astype(jnp.float32)
    factor = lax.rsqrt(jnp.mean(wide * wide, axis=1, keepdims=True) + 1e-05)
    return (wide * factor * gain).astype(jnp.bfloat16)


def tile_stats(normed, labels, head, first):
    total = normed.shape[0]
    block = math.gcd(total, 512)
    columns = first + lax.iota(jnp.int32, head.shape[0])

    def one_block(pair):
        rows, marks = pair
        logits = lax.dot_general(
            rows, head, (((1,), (1,)), ((), ())), preferred_element_type=jnp.float32
        )
        peak = jnp.max(logits, axis=1)
        mass = jnp.sum(jnp.exp(logits - peak[:, None]), axis=1)
        hit = jnp.sum(jnp.where(marks[:, None] == columns[None, :], logits, 0.0), axis=1)
        return (peak, mass, hit)

    peak, mass, hit = lax.map(
        one_block,
        (
            normed.reshape(total // block, block, normed.shape[1]),
            labels.reshape(total // block, block),
        ),
    )
    return (peak.reshape(total), mass.reshape(total), hit.reshape(total))


def shards(hidden, norm_gain, head, targets, route):
    place = lax.axis_index(("dp", "pp"))
    devices = lax.axis_size(("dp", "pp"))
    pipes = lax.axis_size("dp")
    rows = hidden.shape[0]
    gathered, labels = (
        lax.all_gather(hidden, ("dp", "pp"), axis=0, tiled=True),
        lax.all_gather(targets, ("dp", "pp"), axis=0, tiled=True),
    )
    normed = rms_normal(gathered, norm_gain)
    peak, mass, hit = tile_stats(normed, labels, head, place * head.shape[0])
    peak_all, mass_all, hit_all = (
        lax.all_to_all(
            peak.reshape(devices, rows), ("dp", "pp"), split_axis=0, concat_axis=0, tiled=True
        ),
        lax.all_to_all(
            mass.reshape(devices, rows), ("dp", "pp"), split_axis=0, concat_axis=0, tiled=True
        ),
        lax.all_to_all(
            hit.reshape(devices, rows), ("dp", "pp"), split_axis=0, concat_axis=0, tiled=True
        ),
    )
    top = jnp.max(peak_all, axis=0)
    mass_own = jnp.sum(mass_all * jnp.exp(peak_all - top[None, :]), axis=0)
    hit_own = jnp.sum(hit_all, axis=0)
    token_loss = top + jnp.log(mass_own) - hit_own
    mine = route[place]
    credit = jnp.where(lax.iota(jnp.int32, pipes) == mine, jnp.sum(token_loss), 0.0)
    summed = lax.psum(credit, ("dp", "pp"))
    pipe_loss = summed / (rows * devices // pipes)
    return (token_loss, pipe_loss)


def solution(mesh):
    placed = (P(("dp", "pp"), None), P(), P(("dp", "pp"), None), P(("dp", "pp")), P())
    return jax.shard_map(
        shards, mesh=mesh, in_specs=placed, out_specs=(P(("dp", "pp")), P()), check_vma=False
    )
```

profile of v0, /device:TPU:0, one launch (start us, length us, event | category | flops | bytes accessed | tf_op | source)
XLA Modules:
  0.0 165.2 jit_solution(11259137968374212607)
XLA Ops:
  7.2 0.0 copy-start.1
  7.2 0.0 all-gather.2.cloned.1.call-start
  7.2 0.7 all-gather.2.cloned.1.call-update
  7.9 0.9 dynamic-update-slice
  8.8 42.0 %all-reduce = s32[512]{0:T(512)S(1)} all-reduce(s32[512]{0:T(512)S(1)} %dynamic-update-slice), channel_id=1, replica_groups=mesh['dp'=4,'pp'=8] {'dp','pp'}, use_global_device_ids=true, to_apply=%add | all-reduce | flops 512 | bytes 4096
  50.8 24.9 %all-gather.2.cloned.1.call-done = bf16[512,4096]{1,0:T(8,128)(2,1)} async-done(((bf16[16,4096]{1,0:T(8,128)(2,1)}), bf16[512,4096]{1,0:T(8,128)(2,1)}) %all-gather.2.cloned.1.call-update) | async-done | bytes 4194320 | tf_op jit(solution)/shard_map/all_gather | solution.py:45
  75.7 0.0 copy-start
  75.7 3.2 %fusion = f32[512]{0:T(512)S(1)} fusion(bf16[512,4096]{1,0:T(8,128)(2,1)} %all-gather.2.cloned.1.call-done), kind=kLoop, calls=%fused_computation.2 | loop fusion | flops 6290944 | bytes 4196352 | tf_op jit(solution)/shard_map/reduce_sum | solution.py:10
  79.0 0.0 copy-done.1
  79.0 0.2 copy-done
  79.2 0.0 copy-start.2
  79.2 7.4 %fusion.8 = (f32[512]{0:T(512)S(1)}, f32[512,1024]{1,0:T(8,128)S(1)}) fusion(bf16[1024,4096]{1,0:T(8,128)(2,1)} %param.7, bf16[512,4096]{1,0:T(8,128)(2,1)S(1)} %copy-done, f32[4096]{0:T(1024)S(1)} %copy-done.1, f32[512]{0:T(512)S(1)} %add_rsqrt_fusion), kind=kOutput, calls=%fused_computation.17 | convolution fusion | flops 4303879680 | bytes 14700544 | tf_op jit(solution)/shard_map/while/body/eval_jaxpr/dot_general | solution.py:21
  86.6 0.7 all_to_all.22
  87.3 3.4 %all-to-all-start = ((f32[32,1,16]{2,1,0:T(1,128)}), f32[32,1,16]{2,1,0:T(1,128)S(1)}, u32[]{:S(2)}, u32[]{:S(2)}) async-start(f32[32,1,16]{2,1,0:T(1,128)} %bitcast), calls=%async_computation | async-start | bytes 32768 | tf_op jit(solution)/shard_map/all_to_all | solution.py:51
  90.7 0.6 exponential_reduce_fusion
  91.3 0.7 all_to_all.24
  92.0 5.8 %all-to-all-done = f32[32,1,16]{2,1,0:T(1,128)S(1)} async-done(((f32[32,1,16]{2,1,0:T(1,128)}), f32[32,1,16]{2,1,0:T(1,128)S(1)}, u32[]{:S(2)}, u32[]{:S(2)}) %all-to-all-start) | async-done | bytes 2080 | tf_op jit(solution)/shard_map/all_to_all | solution.py:51
  97.9 2.6 %all-to-all-start.1 = ((f32[32,1,16]{2,1,0:T(1,128)}), f32[32,1,16]{2,1,0:T(1,128)S(1)}, u32[]{:S(2)}, u32[]{:S(2)}) async-start(f32[32,1,16]{2,1,0:T(1,128)} %bitcast.1), calls=%async_computation.1 | async-start | bytes 32768 | tf_op jit(solution)/shard_map/all_to_all | solution.py:54
  100.4 0.0 copy-done.2
  100.4 0.6 dynamic_slice.9
  101.1 0.7 all_to_all.28
  101.7 0.1 reduce_max.20
  101.8 5.8 %all-to-all-done.1 = f32[32,1,16]{2,1,0:T(1,128)S(1)} async-done(((f32[32,1,16]{2,1,0:T(1,128)}), f32[32,1,16]{2,1,0:T(1,128)S(1)}, u32[]{:S(2)}, u32[]{:S(2)}) %all-to-all-start.1) | async-done | bytes 2080 | tf_op jit(solution)/shard_map/all_to_all | solution.py:54
  107.6 2.5 %all-to-all-start.2 = ((f32[32,1,16]{2,1,0:T(1,128)}), f32[32,1,16]{2,1,0:T(1,128)S(1)}, u32[]{:S(2)}, u32[]{:S(2)}) async-start(f32[32,1,16]{2,1,0:T(1,128)} %bitcast.4), calls=%async_computation.2 | async-start | bytes 32768 | tf_op jit(solution)/shard_map/all_to_all | solution.py:57
  110.1 7.1 %all-to-all-done.2 = f32[32,1,16]{2,1,0:T(1,128)S(1)} async-done(((f32[32,1,16]{2,1,0:T(1,128)}), f32[32,1,16]{2,1,0:T(1,128)S(1)}, u32[]{:S(2)}, u32[]{:S(2)}) %all-to-all-start.2) | async-done | bytes 2080 | tf_op jit(solution)/shard_map/all_to_all | solution.py:57
  117.2 0.1 reduce_sum.60
  117.3 1.1 fusion.7
  118.4 1.3 compare_select_fusion
  119.7 38.2 %psum.7 = f32[4]{0:T(128)S(1)} all-reduce(f32[4]{0:T(128)S(1)} %compare_select_fusion), channel_id=1, replica_groups=mesh['dp'=4,'pp'=8] {'dp','pp'}, use_global_device_ids=true, to_apply=%region_8.9 | all-reduce | flops 4 | bytes 32 | tf_op jit(solution)/shard_map/psum | solution.py:67
  157.9 0.5 broadcast_multiply_fusion
  (4 shorter events, 0.0 us)
Async XLA Ops:
  7.2 71.8 %copy-start.1 = (f32[4096]{0:T(1024)S(1)}, f32[4096]{0:T(1024)}, u32[]{:S(2)}) copy-start(f32[4096]{0:T(1024)} %param.6) | copy-start | bytes 49156
  7.2 68.6 %all-gather.2.cloned.1.call-start = ((), (), s32[]{:S(2)}) async-start(), calls=%async_computation.3 | async-start | bytes 4325376 | tf_op jit(solution)/shard_map/all_gather | solution.py:45
  75.7 3.4 %copy-start = (bf16[512,4096]{1,0:T(8,128)(2,1)S(1)}, bf16[512,4096]{1,0:T(8,128)(2,1)}, u32[]{:S(2)}) copy-start(bf16[512,4096]{1,0:T(8,128)(2,1)} %all-gather.2.cloned.1.call-done) | copy-start | bytes 12582916
  79.2 21.2 %copy-start.2 = (s32[32]{0:T(128)S(1)}, s32[32]{0:T(128)}, u32[]{:S(2)}) copy-start(s32[32]{0:T(128)} %param.9) | copy-start | bytes 388
  87.3 10.5 %all-to-all-start = ((f32[32,1,16]{2,1,0:T(1,128)}), f32[32,1,16]{2,1,0:T(1,128)S(1)}, u32[]{:S(2)}, u32[]{:S(2)}) async-start(f32[32,1,16]{2,1,0:T(1,128)} %bitcast), calls=%async_computation | async-start | bytes 32768 | tf_op jit(solution)/shard_map/all_to_all | solution.py:51
  97.9 9.7 %all-to-all-start.1 = ((f32[32,1,16]{2,1,0:T(1,128)}), f32[32,1,16]{2,1,0:T(1,128)S(1)}, u32[]{:S(2)}, u32[]{:S(2)}) async-start(f32[32,1,16]{2,1,0:T(1,128)} %bitcast.1), calls=%async_computation.1 | async-start | bytes 32768 | tf_op jit(solution)/shard_map/all_to_all | solution.py:54
  107.6 9.6 %all-to-all-start.2 = ((f32[32,1,16]{2,1,0:T(1,128)}), f32[32,1,16]{2,1,0:T(1,128)S(1)}, u32[]{:S(2)}, u32[]{:S(2)}) async-start(f32[32,1,16]{2,1,0:T(1,128)} %bitcast.4), calls=%async_computation.2 | async-start | bytes 32768 | tf_op jit(solution)/shard_map/all_to_all | solution.py:57
Sparse Core Ops, SparseCore 0:
  11.1 64.6 all-gather.1
where the time goes:
time: 166 us; the launch traced here: 165 us
  blocking collectives  80.3 us (48%)
  waiting for transfers between devices  44.3 us (27%)
  between operations  14.1 us (8%)
  starting transfers between devices  8.47 us (5%)
  matrix products  7.43 us (4%)
  other arithmetic  6.91 us (4%)
  local copies, waits for them, and re-layouts  3.72 us (2%)
    unnamed x1, blocking collectives  42 us
    psum x1, blocking collectives, shards(): summed = lax.psum(credit, ('dp', 'pp'))  38.2 us
    all_gather x1, waiting for transfers between devices, shards(): lax.all_gather(hidden, ('dp', 'pp'), axis=0, tiled=True)  24.9 us
    dot_general x1, matrix products, one_block(): lax.dot_general(rows, head, (((1,), (1,)), ((), ())), preferred_element_t...  7.43 us
    all_to_all x1, waiting for transfers between devices, shards(): lax.all_to_all(hit.reshape(devices, rows), ('dp', 'pp'), split_axis=0, co...  7.12 us
    all_to_all x1, waiting for transfers between devices, shards(): lax.all_to_all(peak.reshape(devices, rows), ('dp', 'pp'), split_axis=0, c...  5.84 us
    all_to_all x1, waiting for transfers between devices, shards(): lax.all_to_all(mass.reshape(devices, rows), ('dp', 'pp'), split_axis=0, c...  5.78 us
    all_to_all x1, starting transfers between devices, shards(): lax.all_to_all(peak.reshape(devices, rows), ('dp', 'pp'), split_axis=0, c...  3.39 us
  transfers between devices with their start and end apart: 4, of which 4 were waited for; matrix products, arithmetic and copies ran while one was open for 1% of the time, Pallas kernels for 0%

commit v1 on v0

--- a/solution.py
+++ b/solution.py
@@ -64,7 +64,7 @@
     token_loss = top + jnp.log(mass_own) - hit_own
     mine = route[place]
     credit = jnp.where(lax.iota(jnp.int32, pipes) == mine, jnp.sum(token_loss), 0.0)
-    summed = lax.psum(credit, ("dp", "pp"))
+    summed = jnp.sum(lax.all_gather(credit, ("dp", "pp")), axis=0)
     pipe_loss = summed / (rows * devices // pipes)
     return (token_loss, pipe_loss)
 

time: 166 us -> 191 us (1.15)
  blocking collectives: 80.3 us -> 106 us
    all_gather x0 -> x1, blocking collectives: none -> 64 us  [shards(): summed = jnp.sum(lax.all_gather(credit, ('dp', 'pp')), axis=0)]
    psum x1 -> x0, blocking collectives: 38.2 us -> none  [shards(): summed = lax.psum(credit, ('dp', 'pp'))]
where the time goes in v1:
time: 191 us
  blocking collectives  106 us (55%)
  waiting for transfers between devices  44.3 us (23%)
  between operations  14.1 us (7%)
  starting transfers between devices  8.47 us (4%)
  matrix products  7.43 us (4%)
  other arithmetic  6.96 us (4%)
  local copies, waits for them, and re-layouts  3.72 us (2%)
    all_gather x1, blocking collectives, shards(): summed = jnp.sum(lax.all_gather(credit, ('dp', 'pp')), axis=0)  64 us
    unnamed x1, blocking collectives  42 us
    all_gather x1, waiting for transfers between devices, shards(): lax.all_gather(hidden, ('dp', 'pp'), axis=0, tiled=True)  24.9 us
    dot_general x1, matrix products, one_block(): lax.dot_general(rows, head, (((1,), (1,)), ((), ())), preferred_element_t...  7.43 us
    all_to_all x1, waiting for transfers between devices, shards(): lax.all_to_all(hit.reshape(devices, rows), ('dp', 'pp'), split_axis=0, co...  7.12 us
    all_to_all x1, waiting for transfers between devices, shards(): lax.all_to_all(peak.reshape(devices, rows), ('dp', 'pp'), split_axis=0, c...  5.84 us
    all_to_all x1, waiting for transfers between devices, shards(): lax.all_to_all(mass.reshape(devices, rows), ('dp', 'pp'), split_axis=0, c...  5.78 us
  transfers between devices with their start and end apart: 4, of which 4 were waited for; matrix products, arithmetic and copies ran while one was open for 1% of the time, Pallas kernels for 0%

profile of v1, /device:TPU:0, one launch (start us, length us, event | category | flops | bytes accessed | tf_op | source)
XLA Modules:
  0.0 191.1 jit_solution(15503443843219503389)
XLA Ops:
  7.2 0.0 copy-start.1
  7.2 0.0 all-gather.3.cloned.1.call-start
  7.2 0.7 all-gather.3.cloned.1.call-update
  7.9 0.9 dynamic-update-slice
  8.8 42.0 %all-reduce = s32[512]{0:T(512)S(1)} all-reduce(s32[512]{0:T(512)S(1)} %dynamic-update-slice), channel_id=1, replica_groups=mesh['dp'=4,'pp'=8] {'dp','pp'}, use_global_device_ids=true, to_apply=%add | all-reduce | flops 512 | bytes 4096
  50.8 24.9 %all-gather.3.cloned.1.call-done = bf16[512,4096]{1,0:T(8,128)(2,1)} async-done(((bf16[16,4096]{1,0:T(8,128)(2,1)}), bf16[512,4096]{1,0:T(8,128)(2,1)}) %all-gather.3.cloned.1.call-update) | async-done | bytes 4194320 | tf_op jit(solution)/shard_map/all_gather | solution.py:45
  75.7 0.0 copy-start
  75.7 3.2 %fusion = f32[512]{0:T(512)S(1)} fusion(bf16[512,4096]{1,0:T(8,128)(2,1)} %all-gather.3.cloned.1.call-done), kind=kLoop, calls=%fused_computation.2 | loop fusion | flops 6290944 | bytes 4196352 | tf_op jit(solution)/shard_map/reduce_sum | solution.py:10
  79.0 0.0 copy-done.1
  79.0 0.2 copy-done
  79.2 0.0 copy-start.2
  79.2 7.4 %fusion.9 = (f32[512]{0:T(512)S(1)}, f32[512,1024]{1,0:T(8,128)S(1)}) fusion(bf16[1024,4096]{1,0:T(8,128)(2,1)} %param.7, bf16[512,4096]{1,0:T(8,128)(2,1)S(1)} %copy-done, f32[4096]{0:T(1024)S(1)} %copy-done.1, f32[512]{0:T(512)S(1)} %add_rsqrt_fusion), kind=kOutput, calls=%fused_computation.18 | convolution fusion | flops 4303879680 | bytes 14700544 | tf_op jit(solution)/shard_map/while/body/eval_jaxpr/dot_general | solution.py:21
  86.6 0.7 all_to_all.22
  87.3 3.4 %all-to-all-start = ((f32[32,1,16]{2,1,0:T(1,128)}), f32[32,1,16]{2,1,0:T(1,128)S(1)}, u32[]{:S(2)}, u32[]{:S(2)}) async-start(f32[32,1,16]{2,1,0:T(1,128)} %bitcast), calls=%async_computation | async-start | bytes 32768 | tf_op jit(solution)/shard_map/all_to_all | solution.py:51
  90.7 0.6 exponential_reduce_fusion
  91.3 0.7 all_to_all.24
  92.0 5.8 %all-to-all-done = f32[32,1,16]{2,1,0:T(1,128)S(1)} async-done(((f32[32,1,16]{2,1,0:T(1,128)}), f32[32,1,16]{2,1,0:T(1,128)S(1)}, u32[]{:S(2)}, u32[]{:S(2)}) %all-to-all-start) | async-done | bytes 2080 | tf_op jit(solution)/shard_map/all_to_all | solution.py:51
  97.9 2.6 %all-to-all-start.1 = ((f32[32,1,16]{2,1,0:T(1,128)}), f32[32,1,16]{2,1,0:T(1,128)S(1)}, u32[]{:S(2)}, u32[]{:S(2)}) async-start(f32[32,1,16]{2,1,0:T(1,128)} %bitcast.1), calls=%async_computation.1 | async-start | bytes 32768 | tf_op jit(solution)/shard_map/all_to_all | solution.py:54
  100.4 0.0 copy-done.2
  100.4 0.6 dynamic_slice.9
  101.1 0.7 all_to_all.28
  101.7 0.1 reduce_max.20
  101.8 5.8 %all-to-all-done.1 = f32[32,1,16]{2,1,0:T(1,128)S(1)} async-done(((f32[32,1,16]{2,1,0:T(1,128)}), f32[32,1,16]{2,1,0:T(1,128)S(1)}, u32[]{:S(2)}, u32[]{:S(2)}) %all-to-all-start.1) | async-done | bytes 2080 | tf_op jit(solution)/shard_map/all_to_all | solution.py:54
  107.6 2.5 %all-to-all-start.2 = ((f32[32,1,16]{2,1,0:T(1,128)}), f32[32,1,16]{2,1,0:T(1,128)S(1)}, u32[]{:S(2)}, u32[]{:S(2)}) async-start(f32[32,1,16]{2,1,0:T(1,128)} %bitcast.4), calls=%async_computation.2 | async-start | bytes 32768 | tf_op jit(solution)/shard_map/all_to_all | solution.py:57
  110.1 7.1 %all-to-all-done.2 = f32[32,1,16]{2,1,0:T(1,128)S(1)} async-done(((f32[32,1,16]{2,1,0:T(1,128)}), f32[32,1,16]{2,1,0:T(1,128)S(1)}, u32[]{:S(2)}, u32[]{:S(2)}) %all-to-all-start.2) | async-done | bytes 2080 | tf_op jit(solution)/shard_map/all_to_all | solution.py:57
  117.2 0.1 reduce_sum.69
  117.3 1.1 fusion.8
  118.4 1.3 fusion.7
  119.7 64.0 %all-gather = f32[32,1,4]{2,1,0:T(1,128)S(1)} all-gather(f32[1,1,4]{2,1,0:T(1,128)S(1)} %fusion.7), channel_id=1, replica_groups=mesh['dp'=4,'pp'=8] {'dp','pp'}, dimensions={0}, use_global_device_ids=true | all-gather | bytes 528 | tf_op jit(solution)/shard_map/all_gather | solution.py:67
  183.6 0.1 reduce_sum.71
  183.7 0.5 broadcast_multiply_fusion
  (4 shorter events, 0.0 us)
Async XLA Ops:
  7.2 71.8 %copy-start.1 = (f32[4096]{0:T(1024)S(1)}, f32[4096]{0:T(1024)}, u32[]{:S(2)}) copy-start(f32[4096]{0:T(1024)} %param.6) | copy-start | bytes 49156
  7.2 68.6 %all-gather.3.cloned.1.call-start = ((), (), s32[]{:S(2)}) async-start(), calls=%async_computation.3 | async-start | bytes 4325376 | tf_op jit(solution)/shard_map/all_gather | solution.py:45
  75.7 3.4 %copy-start = (bf16[512,4096]{1,0:T(8,128)(2,1)S(1)}, bf16[512,4096]{1,0:T(8,128)(2,1)}, u32[]{:S(2)}) copy-start(bf16[512,4096]{1,0:T(8,128)(2,1)} %all-gather.3.cloned.1.call-done) | copy-start | bytes 12582916
  79.2 21.2 %copy-start.2 = (s32[32]{0:T(128)S(1)}, s32[32]{0:T(128)}, u32[]{:S(2)}) copy-start(s32[32]{0:T(128)} %param.9) | copy-start | bytes 388
  87.3 10.5 %all-to-all-start = ((f32[32,1,16]{2,1,0:T(1,128)}), f32[32,1,16]{2,1,0:T(1,128)S(1)}, u32[]{:S(2)}, u32[]{:S(2)}) async-start(f32[32,1,16]{2,1,0:T(1,128)} %bitcast), calls=%async_computation | async-start | bytes 32768 | tf_op jit(solution)/shard_map/all_to_all | solution.py:51
  97.9 9.7 %all-to-all-start.1 = ((f32[32,1,16]{2,1,0:T(1,128)}), f32[32,1,16]{2,1,0:T(1,128)S(1)}, u32[]{:S(2)}, u32[]{:S(2)}) async-start(f32[32,1,16]{2,1,0:T(1,128)} %bitcast.1), calls=%async_computation.1 | async-start | bytes 32768 | tf_op jit(solution)/shard_map/all_to_all | solution.py:54
  107.6 9.6 %all-to-all-start.2 = ((f32[32,1,16]{2,1,0:T(1,128)}), f32[32,1,16]{2,1,0:T(1,128)S(1)}, u32[]{:S(2)}, u32[]{:S(2)}) async-start(f32[32,1,16]{2,1,0:T(1,128)} %bitcast.4), calls=%async_computation.2 | async-start | bytes 32768 | tf_op jit(solution)/shard_map/all_to_all | solution.py:57
Sparse Core Ops, SparseCore 0:
  11.1 64.6 all-gather.2

commit v2 on v0

--- a/solution.py
+++ b/solution.py
@@ -64,7 +64,7 @@
     token_loss = top + jnp.log(mass_own) - hit_own
     mine = route[place]
     credit = jnp.where(lax.iota(jnp.int32, pipes) == mine, jnp.sum(token_loss), 0.0)
-    summed = lax.psum(credit, ("dp", "pp"))
+    summed = lax.psum(lax.psum(credit, "pp"), "dp")
     pipe_loss = summed / (rows * devices // pipes)
     return (token_loss, pipe_loss)
 

time: 166 us -> 151 us (0.910)
  blocking collectives: 80.3 us -> 65.8 us
    psum x1 -> x2, blocking collectives: 38.2 us -> 23.7 us  [shards(): summed = lax.psum(lax.psum(credit, 'pp'), 'dp')]
where the time goes in v2:
time: 151 us
  blocking collectives  65.8 us (44%)
  waiting for transfers between devices  44.3 us (29%)
  between operations  14.1 us (9%)
  starting transfers between devices  8.47 us (6%)
  matrix products  7.43 us (5%)
  other arithmetic  6.91 us (5%)
  local copies, waits for them, and re-layouts  3.72 us (2%)
    unnamed x1, blocking collectives  42 us
    all_gather x1, waiting for transfers between devices, shards(): lax.all_gather(hidden, ('dp', 'pp'), axis=0, tiled=True)  24.9 us
    psum x2, blocking collectives, shards(): summed = lax.psum(lax.psum(credit, 'pp'), 'dp')  23.7 us
    dot_general x1, matrix products, one_block(): lax.dot_general(rows, head, (((1,), (1,)), ((), ())), preferred_element_t...  7.43 us
    all_to_all x1, waiting for transfers between devices, shards(): lax.all_to_all(hit.reshape(devices, rows), ('dp', 'pp'), split_axis=0, co...  7.12 us
    all_to_all x1, waiting for transfers between devices, shards(): lax.all_to_all(peak.reshape(devices, rows), ('dp', 'pp'), split_axis=0, c...  5.84 us
    all_to_all x1, waiting for transfers between devices, shards(): lax.all_to_all(mass.reshape(devices, rows), ('dp', 'pp'), split_axis=0, c...  5.78 us
    all_to_all x1, starting transfers between devices, shards(): lax.all_to_all(peak.reshape(devices, rows), ('dp', 'pp'), split_axis=0, c...  3.39 us
  transfers between devices with their start and end apart: 4, of which 4 were waited for; matrix products, arithmetic and copies ran while one was open for 1% of the time, Pallas kernels for 0%

profile of v2, /device:TPU:0, one launch (start us, length us, event | category | flops | bytes accessed | tf_op | source)
XLA Modules:
  0.0 150.8 jit_solution(356328562407717495)
XLA Ops:
  7.2 0.0 copy-start.1
  7.2 0.0 all-gather.2.cloned.1.call-start
  7.2 0.7 all-gather.2.cloned.1.call-update
  7.9 0.9 dynamic-update-slice
  8.8 42.0 %all-reduce = s32[512]{0:T(512)S(1)} all-reduce(s32[512]{0:T(512)S(1)} %dynamic-update-slice), channel_id=1, replica_groups=mesh['dp'=4,'pp'=8] {'dp','pp'}, use_global_device_ids=true, to_apply=%add | all-reduce | flops 512 | bytes 4096
  50.8 24.9 %all-gather.2.cloned.1.call-done = bf16[512,4096]{1,0:T(8,128)(2,1)} async-done(((bf16[16,4096]{1,0:T(8,128)(2,1)}), bf16[512,4096]{1,0:T(8,128)(2,1)}) %all-gather.2.cloned.1.call-update) | async-done | bytes 4194320 | tf_op jit(solution)/shard_map/all_gather | solution.py:45
  75.7 0.0 copy-start
  75.7 3.2 %fusion = f32[512]{0:T(512)S(1)} fusion(bf16[512,4096]{1,0:T(8,128)(2,1)} %all-gather.2.cloned.1.call-done), kind=kLoop, calls=%fused_computation.2 | loop fusion | flops 6290944 | bytes 4196352 | tf_op jit(solution)/shard_map/reduce_sum | solution.py:10
  79.0 0.0 copy-done.1
  79.0 0.2 copy-done
  79.2 0.0 copy-start.2
  79.2 7.4 %fusion.8 = (f32[512]{0:T(512)S(1)}, f32[512,1024]{1,0:T(8,128)S(1)}) fusion(bf16[1024,4096]{1,0:T(8,128)(2,1)} %param.7, bf16[512,4096]{1,0:T(8,128)(2,1)S(1)} %copy-done, f32[4096]{0:T(1024)S(1)} %copy-done.1, f32[512]{0:T(512)S(1)} %add_rsqrt_fusion), kind=kOutput, calls=%fused_computation.17 | convolution fusion | flops 4303879680 | bytes 14700544 | tf_op jit(solution)/shard_map/while/body/eval_jaxpr/dot_general | solution.py:21
  86.6 0.7 all_to_all.22
  87.3 3.4 %all-to-all-start = ((f32[32,1,16]{2,1,0:T(1,128)}), f32[32,1,16]{2,1,0:T(1,128)S(1)}, u32[]{:S(2)}, u32[]{:S(2)}) async-start(f32[32,1,16]{2,1,0:T(1,128)} %bitcast), calls=%async_computation | async-start | bytes 32768 | tf_op jit(solution)/shard_map/all_to_all | solution.py:51
  90.7 0.6 exponential_reduce_fusion
  91.3 0.7 all_to_all.24
  92.0 5.8 %all-to-all-done = f32[32,1,16]{2,1,0:T(1,128)S(1)} async-done(((f32[32,1,16]{2,1,0:T(1,128)}), f32[32,1,16]{2,1,0:T(1,128)S(1)}, u32[]{:S(2)}, u32[]{:S(2)}) %all-to-all-start) | async-done | bytes 2080 | tf_op jit(solution)/shard_map/all_to_all | solution.py:51
  97.9 2.6 %all-to-all-start.1 = ((f32[32,1,16]{2,1,0:T(1,128)}), f32[32,1,16]{2,1,0:T(1,128)S(1)}, u32[]{:S(2)}, u32[]{:S(2)}) async-start(f32[32,1,16]{2,1,0:T(1,128)} %bitcast.1), calls=%async_computation.1 | async-start | bytes 32768 | tf_op jit(solution)/shard_map/all_to_all | solution.py:54
  100.4 0.0 copy-done.2
  100.4 0.6 dynamic_slice.9
  101.1 0.7 all_to_all.28
  101.7 0.1 reduce_max.20
  101.8 5.8 %all-to-all-done.1 = f32[32,1,16]{2,1,0:T(1,128)S(1)} async-done(((f32[32,1,16]{2,1,0:T(1,128)}), f32[32,1,16]{2,1,0:T(1,128)S(1)}, u32[]{:S(2)}, u32[]{:S(2)}) %all-to-all-start.1) | async-done | bytes 2080 | tf_op jit(solution)/shard_map/all_to_all | solution.py:54
  107.6 2.5 %all-to-all-start.2 = ((f32[32,1,16]{2,1,0:T(1,128)}), f32[32,1,16]{2,1,0:T(1,128)S(1)}, u32[]{:S(2)}, u32[]{:S(2)}) async-start(f32[32,1,16]{2,1,0:T(1,128)} %bitcast.4), calls=%async_computation.2 | async-start | bytes 32768 | tf_op jit(solution)/shard_map/all_to_all | solution.py:57
  110.1 7.1 %all-to-all-done.2 = f32[32,1,16]{2,1,0:T(1,128)S(1)} async-done(((f32[32,1,16]{2,1,0:T(1,128)}), f32[32,1,16]{2,1,0:T(1,128)S(1)}, u32[]{:S(2)}, u32[]{:S(2)}) %all-to-all-start.2) | async-done | bytes 2080 | tf_op jit(solution)/shard_map/all_to_all | solution.py:57
  117.2 0.1 reduce_sum.60
  117.3 1.1 fusion.7
  118.4 1.3 compare_select_fusion
  119.7 17.7 %psum.14 = f32[4]{0:T(128)S(1)} all-reduce(f32[4]{0:T(128)S(1)} %compare_select_fusion), channel_id=1, replica_groups=mesh['dp'=4,'pp'=8] {'pp'}, use_global_device_ids=true, to_apply=%region_8.9 | all-reduce | flops 4 | bytes 32 | tf_op jit(solution)/shard_map/psum | solution.py:67
  137.4 6.0 %psum.15 = f32[4]{0:T(128)S(1)} all-reduce(f32[4]{0:T(128)S(1)} %psum.14), channel_id=1, replica_groups=mesh['dp'=4,'pp'=8] {'dp'}, use_global_device_ids=true, to_apply=%region_9.10 | all-reduce | flops 4 | bytes 32 | tf_op jit(solution)/shard_map/psum | solution.py:67
  143.4 0.5 broadcast_multiply_fusion
  (4 shorter events, 0.0 us)
Async XLA Ops:
  7.2 71.8 %copy-start.1 = (f32[4096]{0:T(1024)S(1)}, f32[4096]{0:T(1024)}, u32[]{:S(2)}) copy-start(f32[4096]{0:T(1024)} %param.6) | copy-start | bytes 49156
  7.2 68.6 %all-gather.2.cloned.1.call-start = ((), (), s32[]{:S(2)}) async-start(), calls=%async_computation.3 | async-start | bytes 4325376 | tf_op jit(solution)/shard_map/all_gather | solution.py:45
  75.7 3.4 %copy-start = (bf16[512,4096]{1,0:T(8,128)(2,1)S(1)}, bf16[512,4096]{1,0:T(8,128)(2,1)}, u32[]{:S(2)}) copy-start(bf16[512,4096]{1,0:T(8,128)(2,1)} %all-gather.2.cloned.1.call-done) | copy-start | bytes 12582916
  79.2 21.2 %copy-start.2 = (s32[32]{0:T(128)S(1)}, s32[32]{0:T(128)}, u32[]{:S(2)}) copy-start(s32[32]{0:T(128)} %param.9) | copy-start | bytes 388
  87.3 10.5 %all-to-all-start = ((f32[32,1,16]{2,1,0:T(1,128)}), f32[32,1,16]{2,1,0:T(1,128)S(1)}, u32[]{:S(2)}, u32[]{:S(2)}) async-start(f32[32,1,16]{2,1,0:T(1,128)} %bitcast), calls=%async_computation | async-start | bytes 32768 | tf_op jit(solution)/shard_map/all_to_all | solution.py:51
  97.9 9.7 %all-to-all-start.1 = ((f32[32,1,16]{2,1,0:T(1,128)}), f32[32,1,16]{2,1,0:T(1,128)S(1)}, u32[]{:S(2)}, u32[]{:S(2)}) async-start(f32[32,1,16]{2,1,0:T(1,128)} %bitcast.1), calls=%async_computation.1 | async-start | bytes 32768 | tf_op jit(solution)/shard_map/all_to_all | solution.py:54
  107.6 9.6 %all-to-all-start.2 = ((f32[32,1,16]{2,1,0:T(1,128)}), f32[32,1,16]{2,1,0:T(1,128)S(1)}, u32[]{:S(2)}, u32[]{:S(2)}) async-start(f32[32,1,16]{2,1,0:T(1,128)} %bitcast.4), calls=%async_computation.2 | async-start | bytes 32768 | tf_op jit(solution)/shard_map/all_to_all | solution.py:57
Sparse Core Ops, SparseCore 0:
  11.1 64.6 all-gather.1
